TPU v7x, 128 devices: a whole 4x4x4 slice. The times are simulated.
128 devices in a mesh: row: 8 (over x, core), col: 16 (over z, y).
Axes of the slice: x: 4, y: 4, z: 4, core: 2. Of those that a mesh axis runs over, the one named last changes fastest.
Arguments:
- spectrum: float32 [2, 33554432], P(None, ('row', 'col')), may hold values from -6 to 6
Outputs:
- product: float32 [2, 33554432], P(None, ('row', 'col'))
All inputs are finite; a program needn't handle non-finite values.
Results may differ from a plain program's by a relative error of at most 0.000098.
Values sent between devices are 32-bit elements; how exact they have to be, the bound alone decides.
A program may use at most 64 MiB of HBM per device.

v0:
```python
import functools
import math

import jax
import jax.numpy as jnp
import numpy as np
from jax import lax
from jax.experimental import pallas as pl
from jax.experimental.pallas import tpu as pltpu
from jax.sharding import PartitionSpec as P

B = 131072
MODES = 33554432
POINTS = 50331648
DEVICES = 128
STEP = 37

MESH = pl.DeviceIdType.MESH
F32 = jnp.float32
BF16 = jnp.bfloat16


def unit(turns, total):
    angle = 2.0 * np.pi * (np.asarray(turns, np.int64) % total) / total
    return np.cos(angle), np.sin(angle)


def tables():
    m = np.arange(128)
    lane = np.arange(128)
    cos, sin = unit(m[:, None] * m[None, :], 128)
    plus = np.block([[cos, -sin], [sin, cos]])
    both = np.stack([plus, plus.T]).astype(np.float32)
    high = both.astype(BF16)
    low = (both - high.astype(np.float32)).astype(BF16)
    lanes = np.zeros((3, 2, 128, 128), np.float32)
    place = np.zeros((3, 2, 128, 128), np.float32)
    columns = np.zeros((4, 128, 128), np.float32)
    for i in range(3):
        mine = i + 3 * m
        lanes[i] = unit(mine[:, None] * lane[None, :], POINTS)
        place[i] = unit(mine[:, None] * lane[None, :] * 1024, POINTS)
        re, im = unit(mine[:, None] * np.arange(8)[None, :] * 128, POINTS)
        columns[i, :, 0:8], columns[i, :, 8:16] = re, im
        columns[i, :, 16], columns[i, :, 17] = unit(i * m, 384)
        columns[i, :, 18], columns[i, :, 19] = unit(i * (m + 256), 384)
    re, im = unit(m[:, None] * np.arange(8)[None, :], 1024)
    columns[3, :, 0:8], columns[3, :, 8:16] = re, im
    inner = np.stack(unit(m[:, None] * lane[None, :], B)).astype(np.float32)
    outer = np.stack(unit(np.arange(8)[:, None] * lane[None, :], 1024)).astype(np.float32)
    return high, low, lanes, place, columns, inner, outer


def split(value):
    high = value.astype(BF16)
    return high, (value - high.astype(F32)).astype(BF16)


def from_left(high, low, value):
    left = jnp.concatenate([high, high, low], axis=1)
    top, rest = split(value)
    right = jnp.concatenate([top, rest, top], axis=0)
    return jnp.dot(left, right, preferred_element_type=F32)


def from_right(value, high, low):
    top, rest = split(value)
    left = jnp.concatenate([top, rest, top], axis=1)
    right = jnp.concatenate([high, high, low], axis=0)
    return jnp.dot(left, right, preferred_element_type=F32)


def times(a, b):
    return a[0] * b[0] - a[1] * b[1], a[0] * b[1] + a[1] * b[0]


def times_conj(a, b):
    return a[0] * b[0] + a[1] * b[1], a[1] * b[0] - a[0] * b[1]


def turn(a, sign):
    return (-a[1], a[0]) if sign > 0 else (a[1], -a[0])


def add(a, b):
    return a[0] + b[0], a[1] + b[1]


def sub(a, b):
    return a[0] - b[0], a[1] - b[1]


def four(a, b, c, d, sign):
    even, odd = add(a, c), sub(a, c)
    other, cross = add(b, d), turn(sub(b, d), sign)
    return add(even, other), add(odd, cross), sub(even, other), sub(odd, cross)


def eight(v, sign):
    even = four(v[0], v[2], v[4], v[6], sign)
    odd = four(v[1], v[3], v[5], v[7], sign)
    half = math.sqrt(0.5)
    one = turn(odd[1], sign)
    one = ((odd[1][0] + one[0]) * half, (odd[1][1] + one[1]) * half)
    two = turn(odd[2], sign)
    three = turn(odd[3], sign)
    three = ((three[0] - odd[3][0]) * half, (three[1] - odd[3][1]) * half)
    odd = (odd[0], one, two, three)
    return [add(e, o) for e, o in zip(even, odd)] + [sub(e, o) for e, o in zip(even, odd)]


def paired(first, second):
    re = jnp.concatenate([first[0], second[0]], axis=1)
    im = jnp.concatenate([first[1], second[1]], axis=1)
    return jnp.concatenate([re, im], axis=0)


def parts(value, which):
    cols = slice(128 * which, 128 * which + 128)
    return value[:128, cols], value[128:, cols]


def kernel(
    x,
    high,
    low,
    lanes,
    place,
    columns,
    inner,
    outer,
    out,
    kept,
    sent,
    field,
    back,
    home,
    final,
    total,
    work,
    turn1,
    turn2,
    turn3,
    start,
    send,
    recv,
):
    row = lax.axis_index("row")
    col = lax.axis_index("col")
    me = row * 16 + col

    def peer(step):
        t = (step * STEP) % 128
        to_row = ((row // 2 + t // 32) % 4) * 2 + (row % 2 + (t // 16) % 2) % 2
        to_col = ((col // 4 + (t // 4) % 4) % 4) * 4 + (col % 4 + t % 4) % 4
        return to_row, to_col, to_row * 16 + to_col

    barrier = pltpu.get_barrier_semaphore()

    def greet(step, carry):
        to_row, to_col, _ = peer(step)
        pl.semaphore_signal(barrier, inc=1, device_id=(to_row, to_col), device_id_type=MESH)
        return carry

    lax.fori_loop(1, DEVICES, greet, 0)
    pl.semaphore_wait(barrier, DEVICES - 1)

    def exchange(src_of, dst_of, phase):
        pltpu.make_async_copy(src_of(me), dst_of(me), recv.at[phase]).start()

        def one(step, carry):
            to_row, to_col, to = peer(step)
            pltpu.make_async_remote_copy(
                src_ref=src_of(to),
                dst_ref=dst_of(me),
                send_sem=send.at[phase],
                recv_sem=recv.at[phase],
                device_id=(to_row, to_col),
                device_id_type=MESH,
            ).start()
            return carry

        lax.fori_loop(1, DEVICES, one, 0)

    def arrived(ref, phase):
        pltpu.make_async_copy(ref, ref, recv.at[phase]).wait()

    def gone(ref, phase):
        pltpu.make_async_copy(ref, ref, send.at[phase]).wait()

    exchange(lambda q: x.at[:, q], lambda p: kept.at[pl.ds(2 * p, 2)], 0)

    here = lax.broadcasted_iota(jnp.int32, (128, 128), 1) == me

    def prepare(i, carry):
        own = [
            jnp.sum(jnp.where(here, place[i, r], 0.0), axis=1, keepdims=True) for r in range(2)
        ]
        base = lanes[i, 0], lanes[i, 1]
        for c in range(8):
            step = columns[i, :, c : c + 1], columns[i, :, 8 + c : 9 + c]
            re, im = times(times(own, step), base)
            turn1[i, c, 0], turn1[i, c, 1] = re, im
        for k in range(4):
            start[i, k] = jnp.broadcast_to(columns[i, :, 16 + k : 17 + k], (128, 128))
        return carry

    lax.fori_loop(0, 3, prepare, 0)
    for s in range(8):
        for r in range(2):
            turn2[s, r] = jnp.broadcast_to(columns[3, :, 8 * r + s : 8 * r + s + 1], (128, 128))
        re, im = times((inner[0], inner[1]), (outer[0, s : s + 1], outer[1, s : s + 1]))
        turn3[s, 0], turn3[s, 1] = re, im
    total[...] = jnp.zeros_like(total)

    kept_rows = kept.reshape(4096, 128)
    sent_rows = sent.reshape(3, 2048, 128)
    field_rows = field.reshape(3, 2, 1024, 128)
    back_rows = back.reshape(3, 2048, 128)
    home_rows = home.reshape(3, 2048, 128)
    final_rows = final.reshape(4096, 128)

    def every(first, gap):
        return pl.ds(first, 128, stride=gap)

    arrived(kept, 0)

    def expand(i, carry):
        by_low = start[i, 0], start[i, 1]
        by_high = start[i, 2], start[i, 3]
        for g in range(4):
            pair = []
            for c in (2 * g, 2 * g + 1):
                below = kept_rows[every(2 * c, 16), :], kept_rows[every(2 * c + 1, 16), :]
                above = (
                    kept_rows[every(2048 + 2 * c, 16), :],
                    kept_rows[every(2049 + 2 * c, 16), :],
                )
                pair.append(add(times(below, by_low), times(above, by_high)))
            mixed = from_left(high[0], low[0], paired(*pair))
            for w in range(2):
                c = 2 * g + w
                re, im = times(parts(mixed, w), (turn1[i, c, 0], turn1[i, c, 1]))
                sent_rows[i, every(c, 16), :] = re
                sent_rows[i, every(8 + c, 16), :] = im
        exchange(lambda q: sent.at[i, q], lambda p: field.at[i, :, p], 1 + i)
        return carry

    lax.fori_loop(0, 3, expand, 0)

    scale = 1.0 / math.sqrt(MODES)
    factor = 1.0 / math.sqrt(POINTS)

    def middle(i, carry):
        arrived(field.at[i], 1 + i)
        for g in range(4):
            pair = [
                (field_rows[i, 0, every(s, 8), :], field_rows[i, 1, every(s, 8), :])
                for s in (2 * g, 2 * g + 1)
            ]
            mixed = from_left(high[0], low[0], paired(*pair))
            for w in range(2):
                work[2 * g + w, 0], work[2 * g + w, 1] = parts(mixed, w)

        def rise(k, inside):
            rows = pl.ds(pl.multiple_of(8 * k, 8), 8)
            v = [
                times(
                    (work[s, 0, rows, :], work[s, 1, rows, :]),
                    (turn2[s, 0, rows, :], turn2[s, 1, rows, :]),
                )
                for s in range(8)
            ]
            v = eight(v, 1)
            for s in range(8):
                re, im = times(v[s], (turn3[s, 0, rows, :], turn3[s, 1, rows, :]))
                work[s, 0, rows, :] = re
                work[s, 1, rows, :] = im
            return inside

        lax.fori_loop(0, 16, rise, 0)

        def peak(k, inside):
            some = pl.ds(4 * k, 4)
            value = jnp.concatenate(
                [work[some, 0].reshape(512, 128), work[some, 1].reshape(512, 128)], axis=1
            )
            value = from_right(value, high[1], low[1]) * scale
            re, im = value[:, :128], value[:, 128:]
            value = jnp.concatenate(
                [(re * re - im * im) * factor, (2.0 * factor) * (re * im)], axis=1
            )
            value = from_right(value, high[0], low[0])
            re, im = times_conj(
                (value[:, :128].reshape(4, 128, 128), value[:, 128:].reshape(4, 128, 128)),
                (turn3[some, 0], turn3[some, 1]),
            )
            work[some, 0] = re
            work[some, 1] = im
            return inside

        lax.fori_loop(0, 2, peak, 0)

        def fall(k, inside):
            rows = pl.ds(pl.multiple_of(8 * k, 8), 8)
            v = eight([(work[s, 0, rows, :], work[s, 1, rows, :]) for s in range(8)], -1)
            for s in range(8):
                re, im = times_conj(v[s], (turn2[s, 0, rows, :], turn2[s, 1, rows, :]))
                work[s, 0, rows, :] = re
                work[s, 1, rows, :] = im
            return inside

        lax.fori_loop(0, 16, fall, 0)
        for g in range(4):
            pair = [(work[s, 0], work[s, 1]) for s in (2 * g, 2 * g + 1)]
            mixed = from_left(high[1], low[1], paired(*pair))
            for w in range(2):
                s = 2 * g + w
                re, im = parts(mixed, w)
                back_rows[i, every(s, 16), :] = re
                back_rows[i, every(8 + s, 16), :] = im
        exchange(lambda q: back.at[i, q], lambda p: home.at[i, p], 4 + i)
        return carry

    lax.fori_loop(0, 3, middle, 0)

    def gather(i, carry):
        arrived(home.at[i], 4 + i)
        by_low = start[i, 0], start[i, 1]
        by_high = start[i, 2], start[i, 3]
        for g in range(4):
            pair = [
                times_conj(
                    (home_rows[i, every(c, 16), :], home_rows[i, every(8 + c, 16), :]),
                    (turn1[i, c, 0], turn1[i, c, 1]),
                )
                for c in (2 * g, 2 * g + 1)
            ]
            mixed = from_left(high[1], low[1], paired(*pair))
            for w in range(2):
                c = 2 * g + w
                value = parts(mixed, w)
                for h, by in enumerate((by_low, by_high)):
                    re, im = times_conj(value, by)
                    total[c, h, 0] += re
                    total[c, h, 1] += im
        return carry

    lax.fori_loop(0, 3, gather, 0)
    for c in range(8):
        for h in range(2):
            for r in range(2):
                final_rows[every(2048 * h + 2 * c + r, 16), :] = total[c, h, r]
    exchange(lambda q: final.at[pl.ds(2 * q, 2)], lambda p: out.at[:, p], 7)
    others = pl.ds(0, DEVICES - 1)
    gone(x.at[:, others], 0)
    for i in range(3):
        gone(sent.at[i, others], 1 + i)
        gone(back.at[i, others], 4 + i)
    arrived(out, 7)
    gone(final.at[pl.ds(0, 2 * (DEVICES - 1))], 7)


def body(spectrum):
    x = spectrum.reshape(2, 2048, 128).transpose(1, 0, 2).reshape(2, 128, 16, 128)
    vmem = pl.BlockSpec(memory_space=pltpu.VMEM)
    anywhere = pl.BlockSpec(memory_space=pl.ANY)
    out = pl.pallas_call(
        kernel,
        name="convolve",
        out_shape=jax.ShapeDtypeStruct((2, 128, 16, 128), F32),
        in_specs=[anywhere] + [vmem] * 7,
        out_specs=anywhere,
        scratch_shapes=[
            pltpu.VMEM((256, 16, 128), F32),
            pltpu.VMEM((3, 128, 2, 8, 128), F32),
            pltpu.VMEM((3, 2, 128, 8, 128), F32),
            pltpu.VMEM((3, 128, 2, 8, 128), F32),
            pltpu.VMEM((3, 128, 2, 8, 128), F32),
            pltpu.VMEM((256, 16, 128), F32),
            pltpu.VMEM((8, 2, 2, 128, 128), F32),
            pltpu.VMEM((8, 2, 128, 128), F32),
            pltpu.VMEM((3, 8, 2, 128, 128), F32),
            pltpu.VMEM((8, 2, 128, 128), F32),
            pltpu.VMEM((8, 2, 128, 128), F32),
            pltpu.VMEM((3, 4, 128, 128), F32),
            pltpu.SemaphoreType.DMA((8,)),
            pltpu.SemaphoreType.DMA((8,)),
        ],
        compiler_params=pltpu.CompilerParams(
            collective_id=0, has_side_effects=True, vmem_limit_bytes=56 * 1024 * 1024
        ),
    )(x, *[jnp.asarray(t) for t in tables()])
    return out.reshape(2048, 2, 128).transpose(1, 0, 2).reshape(2, 262144)


def solution(mesh):
    return jax.shard_map(
        body,
        mesh=mesh,
        in_specs=(P(None, ("row", "col")),),
        out_specs=P(None, ("row", "col")),
        check_vma=False,
    )
```

profile of v0, /device:TPU:1, one launch (start us, length us, event | category | flops | bytes accessed | tf_op | source)
XLA Modules:
  0.0 149.5 jit_solution(18196148528640440957)
XLA Ops:
  0.0 146.8 %convolve.1 = f32[2,128,16,128]{3,2,1,0:T(8,128)} custom-call(f32[2,128,16,128]{3,2,1,0:T(8,128)} %bitcast.11, bf16[2,256,256]{2,1,0:T(8,128)(2,1)} %constant.14.clone.high, bf16[2,256,256]{2,1,0:T(8,128)(2,1)} %constant.15.clone.low, f32[3,2,128,128]{3,2,1,0:T(8,128)} %constant.16.clone.lanes, f32[3,2,128,128]{3,2,1,0:T(8,128)} %constant.17.clone.place, ...), custom_call_target="tpu_custom_call" | custom-call | tf_op jit(solution)/shard_map/convolve/pallas_call | solution.py:368
  146.8 2.6 %copy.12 = f32[2,262144]{1,0:T(2,128)} copy(f32[2,262144]{1,0:T(2,128)} %bitcast.10) | data formatting | bytes 4194304
where the time goes:
time: 150 us; the launch traced here: 149 us
  Pallas kernels  147 us (98%)
  local copies, waits for them, and re-layouts  2.61 us (2%)
    pallas_call x1, Pallas kernels, body(): pl.pallas_call(kernel, name='convolve', out_shape=jax.ShapeDtypeStruct((2...  147 us

commit v1 on v0

--- a/solution.py
+++ b/solution.py
@@ -120,7 +120,20 @@
     return value[:128, cols], value[128:, cols]
 
 
+def wrap(value, size):
+    return jnp.where(value >= size, value - size, value)
+
+
 def kernel(
+    x_far,
+    high_far,
+    low_far,
+    lanes_far,
+    place_far,
+    columns_far,
+    inner_far,
+    outer_far,
+    out,
     x,
     high,
     low,
@@ -129,7 +142,6 @@
     columns,
     inner,
     outer,
-    out,
     kept,
     sent,
     field,
@@ -142,6 +154,7 @@
     turn2,
     turn3,
     start,
+    load,
     send,
     recv,
 ):
@@ -149,38 +162,63 @@
     col = lax.axis_index("col")
     me = row * 16 + col
 
-    def peer(step):
-        t = (step * STEP) % 128
-        to_row = ((row // 2 + t // 32) % 4) * 2 + (row % 2 + (t // 16) % 2) % 2
-        to_col = ((col // 4 + (t // 4) % 4) % 4) * 4 + (col % 4 + t % 4) % 4
-        return to_row, to_col, to_row * 16 + to_col
+    loads = [
+        pltpu.make_async_copy(far, near, load.at[k])
+        for k, (far, near) in enumerate(
+            (
+                (x_far, x),
+                (high_far, high),
+                (low_far, low),
+                (lanes_far, lanes),
+                (place_far, place),
+                (columns_far, columns),
+                (inner_far, inner),
+                (outer_far, outer),
+            )
+        )
+    ]
+    for one in loads:
+        one.start()
+
+    cols = [wrap(col + c, 16) for c in range(16)]
+
+    def each_peer(act):
+        def group(o, base):
+            rows = [wrap(base + k, 8) for k in range(8)]
+            for u in range(16):
+                to_row, to_col = rows[(STEP * u // 16) % 8], cols[STEP * u % 16]
+                if u == 0:
+                    pl.when(o > 0)(functools.partial(act, to_row, to_col))
+                else:
+                    act(to_row, to_col)
+            return wrap(base + STEP % 8, 8)
+
+        lax.fori_loop(0, 8, group, row)
 
     barrier = pltpu.get_barrier_semaphore()
 
-    def greet(step, carry):
-        to_row, to_col, _ = peer(step)
+    def greet(to_row, to_col):
         pl.semaphore_signal(barrier, inc=1, device_id=(to_row, to_col), device_id_type=MESH)
-        return carry
-
-    lax.fori_loop(1, DEVICES, greet, 0)
+
+    each_peer(greet)
+    loads[0].wait()
     pl.semaphore_wait(barrier, DEVICES - 1)
 
     def exchange(src_of, dst_of, phase):
-        pltpu.make_async_copy(src_of(me), dst_of(me), recv.at[phase]).start()
-
-        def one(step, carry):
-            to_row, to_col, to = peer(step)
+        mine = dst_of(me)
+
+        def one(to_row, to_col):
             pltpu.make_async_remote_copy(
-                src_ref=src_of(to),
-                dst_ref=dst_of(me),
+                src_ref=src_of(to_row * 16 + to_col),
+                dst_ref=mine,
                 send_sem=send.at[phase],
                 recv_sem=recv.at[phase],
                 device_id=(to_row, to_col),
                 device_id_type=MESH,
             ).start()
-            return carry
-
-        lax.fori_loop(1, DEVICES, one, 0)
+
+        each_peer(one)
+        pltpu.make_async_copy(src_of(me), mine, recv.at[phase]).start()
 
     def arrived(ref, phase):
         pltpu.make_async_copy(ref, ref, recv.at[phase]).wait()
@@ -188,7 +226,14 @@
     def gone(ref, phase):
         pltpu.make_async_copy(ref, ref, send.at[phase]).wait()
 
-    exchange(lambda q: x.at[:, q], lambda p: kept.at[pl.ds(2 * p, 2)], 0)
+    def first(h, carry):
+        some = pl.ds(pl.multiple_of(8 * h, 8), 8)
+        exchange(lambda q: x.at[:, q, some], lambda p: kept.at[h, pl.ds(2 * p, 2)], h)
+        return carry
+
+    lax.fori_loop(0, 2, first, 0)
+    for one in loads[1:]:
+        one.wait()
 
     here = lax.broadcasted_iota(jnp.int32, (128, 128), 1) == me
 
@@ -213,54 +258,60 @@
         turn3[s, 0], turn3[s, 1] = re, im
     total[...] = jnp.zeros_like(total)
 
-    kept_rows = kept.reshape(4096, 128)
-    sent_rows = sent.reshape(3, 2048, 128)
+    kept_rows = kept.reshape(2, 2048, 128)
+    sent_rows = sent.reshape(3, 2, 1024, 128)
     field_rows = field.reshape(3, 2, 1024, 128)
-    back_rows = back.reshape(3, 2048, 128)
-    home_rows = home.reshape(3, 2048, 128)
-    final_rows = final.reshape(4096, 128)
-
-    def every(first, gap):
-        return pl.ds(first, 128, stride=gap)
-
-    arrived(kept, 0)
-
-    def expand(i, carry):
+    back_rows = back.reshape(3, 2, 1024, 128)
+    home_rows = home.reshape(3, 2, 1024, 128)
+    final_rows = final.reshape(2, 2048, 128)
+
+    def every(first_row):
+        return pl.ds(first_row, 128, stride=8)
+
+    def expand(j, carry):
+        i, h = lax.div(j, 2), lax.rem(j, 2)
+
+        @pl.when(j < 2)
+        def _():
+            arrived(kept.at[h], h)
+
         by_low = start[i, 0], start[i, 1]
         by_high = start[i, 2], start[i, 3]
-        for g in range(4):
+        for g in range(2):
             pair = []
             for c in (2 * g, 2 * g + 1):
-                below = kept_rows[every(2 * c, 16), :], kept_rows[every(2 * c + 1, 16), :]
+                below = kept_rows[h, every(2 * c), :], kept_rows[h, every(2 * c + 1), :]
                 above = (
-                    kept_rows[every(2048 + 2 * c, 16), :],
-                    kept_rows[every(2049 + 2 * c, 16), :],
+                    kept_rows[h, every(1024 + 2 * c), :],
+                    kept_rows[h, every(1025 + 2 * c), :],
                 )
                 pair.append(add(times(below, by_low), times(above, by_high)))
             mixed = from_left(high[0], low[0], paired(*pair))
             for w in range(2):
                 c = 2 * g + w
-                re, im = times(parts(mixed, w), (turn1[i, c, 0], turn1[i, c, 1]))
-                sent_rows[i, every(c, 16), :] = re
-                sent_rows[i, every(8 + c, 16), :] = im
-        exchange(lambda q: sent.at[i, q], lambda p: field.at[i, :, p], 1 + i)
+                by = turn1[i, 4 * h + c, 0], turn1[i, 4 * h + c, 1]
+                re, im = times(parts(mixed, w), by)
+                sent_rows[i, h, every(c), :] = re
+                sent_rows[i, h, every(4 + c), :] = im
+        exchange(lambda q: sent.at[i, h, q], lambda p: field.at[i, h, p], 2 + j)
         return carry
 
-    lax.fori_loop(0, 3, expand, 0)
+    lax.fori_loop(0, 6, expand, 0)
 
     scale = 1.0 / math.sqrt(MODES)
-    factor = 1.0 / math.sqrt(POINTS)
 
     def middle(i, carry):
-        arrived(field.at[i], 1 + i)
-        for g in range(4):
-            pair = [
-                (field_rows[i, 0, every(s, 8), :], field_rows[i, 1, every(s, 8), :])
-                for s in (2 * g, 2 * g + 1)
-            ]
-            mixed = from_left(high[0], low[0], paired(*pair))
-            for w in range(2):
-                work[2 * g + w, 0], work[2 * g + w, 1] = parts(mixed, w)
+        for h in range(2):
+            arrived(field.at[i, h], 2 + 2 * i + h)
+            for g in range(2):
+                pair = [
+                    (field_rows[i, h, every(s), :], field_rows[i, h, every(4 + s), :])
+                    for s in (2 * g, 2 * g + 1)
+                ]
+                mixed = from_left(high[0], low[0], paired(*pair))
+                for w in range(2):
+                    s = 4 * h + 2 * g + w
+                    work[s, 0], work[s, 1] = parts(mixed, w)
 
         def rise(k, inside):
             rows = pl.ds(pl.multiple_of(8 * k, 8), 8)
@@ -287,9 +338,7 @@
             )
             value = from_right(value, high[1], low[1]) * scale
             re, im = value[:, :128], value[:, 128:]
-            value = jnp.concatenate(
-                [(re * re - im * im) * factor, (2.0 * factor) * (re * im)], axis=1
-            )
+            value = jnp.concatenate([re * re - im * im, 2.0 * (re * im)], axis=1)
             value = from_right(value, high[0], low[0])
             re, im = times_conj(
                 (value[:, :128].reshape(4, 128, 128), value[:, 128:].reshape(4, 128, 128)),
@@ -311,28 +360,34 @@
             return inside
 
         lax.fori_loop(0, 16, fall, 0)
-        for g in range(4):
-            pair = [(work[s, 0], work[s, 1]) for s in (2 * g, 2 * g + 1)]
-            mixed = from_left(high[1], low[1], paired(*pair))
-            for w in range(2):
-                s = 2 * g + w
-                re, im = parts(mixed, w)
-                back_rows[i, every(s, 16), :] = re
-                back_rows[i, every(8 + s, 16), :] = im
-        exchange(lambda q: back.at[i, q], lambda p: home.at[i, p], 4 + i)
+
+        def part(h, inside):
+            for g in range(2):
+                pair = [(work[4 * h + s, 0], work[4 * h + s, 1]) for s in (2 * g, 2 * g + 1)]
+                mixed = from_left(high[1], low[1], paired(*pair))
+                for w in range(2):
+                    s = 2 * g + w
+                    re, im = parts(mixed, w)
+                    back_rows[i, h, every(s), :] = re
+                    back_rows[i, h, every(4 + s), :] = im
+            exchange(lambda q: back.at[i, h, q], lambda p: home.at[i, h, p], 8 + 2 * i + h)
+            return inside
+
+        lax.fori_loop(0, 2, part, 0)
         return carry
 
     lax.fori_loop(0, 3, middle, 0)
 
-    def gather(i, carry):
-        arrived(home.at[i], 4 + i)
+    def gather(j, carry):
+        i, h = lax.div(j, 2), lax.rem(j, 2)
+        arrived(home.at[i, h], 8 + j)
         by_low = start[i, 0], start[i, 1]
         by_high = start[i, 2], start[i, 3]
-        for g in range(4):
+        for g in range(2):
             pair = [
                 times_conj(
-                    (home_rows[i, every(c, 16), :], home_rows[i, every(8 + c, 16), :]),
-                    (turn1[i, c, 0], turn1[i, c, 1]),
+                    (home_rows[i, h, every(c), :], home_rows[i, h, every(4 + c), :]),
+                    (turn1[i, 4 * h + c, 0], turn1[i, 4 * h + c, 1]),
                 )
                 for c in (2 * g, 2 * g + 1)
             ]
@@ -340,57 +395,72 @@
             for w in range(2):
                 c = 2 * g + w
                 value = parts(mixed, w)
-                for h, by in enumerate((by_low, by_high)):
+                for f, by in enumerate((by_low, by_high)):
                     re, im = times_conj(value, by)
-                    total[c, h, 0] += re
-                    total[c, h, 1] += im
+                    total[h, c, f, 0] += re
+                    total[h, c, f, 1] += im
+
+        @pl.when(i == 2)
+        def _():
+            for c in range(4):
+                for f in range(2):
+                    for r in range(2):
+                        final_rows[h, every(1024 * f + 2 * c + r), :] = total[h, c, f, r]
+            some = pl.ds(pl.multiple_of(8 * h, 8), 8)
+            exchange(
+                lambda q: final.at[h, pl.ds(2 * q, 2)], lambda p: out.at[:, p, some], 14 + h
+            )
+
         return carry
 
-    lax.fori_loop(0, 3, gather, 0)
-    for c in range(8):
-        for h in range(2):
-            for r in range(2):
-                final_rows[every(2048 * h + 2 * c + r, 16), :] = total[c, h, r]
-    exchange(lambda q: final.at[pl.ds(2 * q, 2)], lambda p: out.at[:, p], 7)
+    lax.fori_loop(0, 6, gather, 0)
     others = pl.ds(0, DEVICES - 1)
-    gone(x.at[:, others], 0)
-    for i in range(3):
-        gone(sent.at[i, others], 1 + i)
-        gone(back.at[i, others], 4 + i)
-    arrived(out, 7)
-    gone(final.at[pl.ds(0, 2 * (DEVICES - 1))], 7)
+    double = pl.ds(0, 2 * (DEVICES - 1))
+    for h in range(2):
+        gone(kept.at[h, double], h)
+        for i in range(3):
+            gone(sent.at[i, h, others], 2 + 2 * i + h)
+            gone(back.at[i, h, others], 8 + 2 * i + h)
+    for h in range(2):
+        arrived(final.at[h], 14 + h)
+        gone(final.at[h, double], 14 + h)
 
 
 def body(spectrum):
     x = spectrum.reshape(2, 2048, 128).transpose(1, 0, 2).reshape(2, 128, 16, 128)
-    vmem = pl.BlockSpec(memory_space=pltpu.VMEM)
     anywhere = pl.BlockSpec(memory_space=pl.ANY)
+    held = [jnp.asarray(t) for t in tables()]
+    grid = (3, 2, 128, 8, 128)
     out = pl.pallas_call(
         kernel,
         name="convolve",
         out_shape=jax.ShapeDtypeStruct((2, 128, 16, 128), F32),
-        in_specs=[anywhere] + [vmem] * 7,
+        in_specs=[anywhere] * (1 + len(held)),
         out_specs=anywhere,
         scratch_shapes=[
-            pltpu.VMEM((256, 16, 128), F32),
-            pltpu.VMEM((3, 128, 2, 8, 128), F32),
-            pltpu.VMEM((3, 2, 128, 8, 128), F32),
-            pltpu.VMEM((3, 128, 2, 8, 128), F32),
-            pltpu.VMEM((3, 128, 2, 8, 128), F32),
-            pltpu.VMEM((256, 16, 128), F32),
-            pltpu.VMEM((8, 2, 2, 128, 128), F32),
+            pltpu.VMEM((2, 128, 16, 128), F32),
+            *[pltpu.VMEM(t.shape, t.dtype) for t in held],
+            pltpu.VMEM((2, 256, 8, 128), F32),
+            pltpu.VMEM(grid, F32),
+            pltpu.VMEM(grid, F32),
+            pltpu.VMEM(grid, F32),
+            pltpu.VMEM(grid, F32),
+            pltpu.VMEM((2, 256, 8, 128), F32),
+            pltpu.VMEM((2, 4, 2, 2, 128, 128), F32),
             pltpu.VMEM((8, 2, 128, 128), F32),
             pltpu.VMEM((3, 8, 2, 128, 128), F32),
             pltpu.VMEM((8, 2, 128, 128), F32),
             pltpu.VMEM((8, 2, 128, 128), F32),
             pltpu.VMEM((3, 4, 128, 128), F32),
             pltpu.SemaphoreType.DMA((8,)),
-            pltpu.SemaphoreType.DMA((8,)),
+            pltpu.SemaphoreType.DMA((16,)),
+            pltpu.SemaphoreType.DMA((16,)),
         ],
         compiler_params=pltpu.CompilerParams(
             collective_id=0, has_side_effects=True, vmem_limit_bytes=56 * 1024 * 1024
         ),
-    )(x, *[jnp.asarray(t) for t in tables()])
+    )(x, *held)
+    out = out * F32(1.0 / math.sqrt(POINTS))
     return out.reshape(2048, 2, 128).transpose(1, 0, 2).reshape(2, 262144)
 
 

time: 150 us -> 132 us (0.88)
  Pallas kernels: 147 us -> 129 us
  other arithmetic: 0 us -> 3.09 us
  local copies, waits for them, and re-layouts: 2.61 us -> 0 us
    pallas_call x1, Pallas kernels: 147 us -> 129 us  [body(): pl.pallas_call(kernel, name='convolve', out_shape=jax.ShapeDtypeStruct((2...]
    mul x0 -> x1, other arithmetic: none -> 3.09 us  [body(): out = out * F32(1.0 / math.sqrt(POINTS))]
    unnamed x1 -> x0, local copies, waits for them, and re-layouts: 2.61 us -> none
where the time goes in v1:
time: 132 us
  Pallas kernels  129 us (98%)
  other arithmetic  3.09 us (2%)
    pallas_call x1, Pallas kernels, body(): pl.pallas_call(kernel, name='convolve', out_shape=jax.ShapeDtypeStruct((2...  129 us
    mul x1, other arithmetic, body(): out = out * F32(1.0 / math.sqrt(POINTS))  3.09 us

profile of v1, /device:TPU:1, one launch (start us, length us, event | category | flops | bytes accessed | tf_op | source)
XLA Modules:
  0.0 132.0 jit_solution(5362365569326531975)
XLA Ops:
  0.0 128.9 %convolve.1 = f32[2,128,16,128]{3,2,1,0:T(8,128)} custom-call(f32[2,128,16,128]{3,2,1,0:T(8,128)} %bitcast.10, bf16[2,256,256]{2,1,0:T(8,128)(2,1)} %constant.16.clone.high_far, bf16[2,256,256]{2,1,0:T(8,128)(2,1)} %constant.17.clone.low_far, f32[3,2,128,128]{3,2,1,0:T(8,128)} %constant.18.clone.lanes_far, f32[3,2,128,128]{3,2,1,0:T(8,128)} %constant.19.clone.place_far, ...), custom_call_target="tpu_custom_call" | custom-call | tf_op jit(solution)/shard_map/convolve/pallas_call | solution.py:434
  128.9 3.1 %broadcast_multiply_fusion = f32[2,128,16,128]{3,2,1,0:T(8,128)} fusion(f32[2,128,16,128]{3,2,1,0:T(8,128)} %convolve.1), kind=kLoop, calls=%fused_computation | loop fusion | flops 524288 | bytes 4194304 | tf_op jit(solution)/shard_map/mul | solution.py:463

commit v2 on v1

--- a/solution.py
+++ b/solution.py
@@ -14,6 +14,16 @@
 POINTS = 50331648
 DEVICES = 128
 STEP = 37
+
+
+def far_to_near():
+    hops = [0, 1, 2, 1]
+    steps = [(STEP * k) % 128 for k in range(1, DEVICES)]
+    steps = [(t // 32, t // 16 % 2, t // 4 % 4, t % 4) for t in steps]
+    return sorted(steps, key=lambda t: -(hops[t[0]] + hops[t[2]] + hops[t[3]]))
+
+
+FAR = far_to_near()
 
 MESH = pl.DeviceIdType.MESH
 F32 = jnp.float32
@@ -195,16 +205,27 @@
 
         lax.fori_loop(0, 8, group, row)
 
+    at_x, at_core = lax.div(row, 2), lax.rem(row, 2)
+    at_z, at_y = lax.div(col, 4), lax.rem(col, 4)
+    to_x = [wrap(at_x + d, 4) * 2 for d in range(4)]
+    to_core = [wrap(at_core + d, 2) for d in range(2)]
+    to_z = [wrap(at_z + d, 4) * 4 for d in range(4)]
+    to_y = [wrap(at_y + d, 4) for d in range(4)]
+
+    def far_first(act):
+        for dx, dc, dz, dy in FAR:
+            act(to_x[dx] + to_core[dc], to_z[dz] + to_y[dy])
+
     barrier = pltpu.get_barrier_semaphore()
 
     def greet(to_row, to_col):
         pl.semaphore_signal(barrier, inc=1, device_id=(to_row, to_col), device_id_type=MESH)
 
-    each_peer(greet)
+    far_first(greet)
     loads[0].wait()
     pl.semaphore_wait(barrier, DEVICES - 1)
 
-    def exchange(src_of, dst_of, phase):
+    def exchange(src_of, dst_of, phase, order=each_peer):
         mine = dst_of(me)
 
         def one(to_row, to_col):
@@ -217,7 +238,7 @@
                 device_id_type=MESH,
             ).start()
 
-        each_peer(one)
+        order(one)
         pltpu.make_async_copy(src_of(me), mine, recv.at[phase]).start()
 
     def arrived(ref, phase):
@@ -299,6 +320,7 @@
     lax.fori_loop(0, 6, expand, 0)
 
     scale = 1.0 / math.sqrt(MODES)
+    factor = 1.0 / math.sqrt(POINTS)
 
     def middle(i, carry):
         for h in range(2):
@@ -338,7 +360,9 @@
             )
             value = from_right(value, high[1], low[1]) * scale
             re, im = value[:, :128], value[:, 128:]
-            value = jnp.concatenate([re * re - im * im, 2.0 * (re * im)], axis=1)
+            value = jnp.concatenate(
+                [(re * re - im * im) * factor, (2.0 * factor) * (re * im)], axis=1
+            )
             value = from_right(value, high[0], low[0])
             re, im = times_conj(
                 (value[:, :128].reshape(4, 128, 128), value[:, 128:].reshape(4, 128, 128)),
@@ -408,7 +432,10 @@
                         final_rows[h, every(1024 * f + 2 * c + r), :] = total[h, c, f, r]
             some = pl.ds(pl.multiple_of(8 * h, 8), 8)
             exchange(
-                lambda q: final.at[h, pl.ds(2 * q, 2)], lambda p: out.at[:, p, some], 14 + h
+                lambda q: final.at[h, pl.ds(2 * q, 2)],
+                lambda p: out.at[:, p, some],
+                14 + h,
+                far_first,
             )
 
         return carry
@@ -434,7 +461,7 @@
     out = pl.pallas_call(
         kernel,
         name="convolve",
-        out_shape=jax.ShapeDtypeStruct((2, 128, 16, 128), F32),
+        out_shape=pltpu.VMEM((2, 128, 16, 128), F32),
         in_specs=[anywhere] * (1 + len(held)),
         out_specs=anywhere,
         scratch_shapes=[
@@ -457,10 +484,9 @@
             pltpu.SemaphoreType.DMA((16,)),
         ],
         compiler_params=pltpu.CompilerParams(
-            collective_id=0, has_side_effects=True, vmem_limit_bytes=56 * 1024 * 1024
+            collective_id=0, has_side_effects=True, vmem_limit_bytes=40 * 1024 * 1024
         ),
-    )(x, *held)
-    out = out * F32(1.0 / math.sqrt(POINTS))
+    )(*[pltpu.with_memory_space_constraint(t, pltpu.HBM) for t in (x, *held)])
     return out.reshape(2048, 2, 128).transpose(1, 0, 2).reshape(2, 262144)
 
 

time: 132 us -> 128 us (0.970)
  other arithmetic: 3.09 us -> 0 us
  Pallas kernels: 129 us -> 127 us
  local copies, waits for them, and re-layouts: 0 us -> 1.32 us
    mul x1 -> x0, other arithmetic: 3.09 us -> none  [body(): out = out * F32(1.0 / math.sqrt(POINTS))]
    pallas_call x1, Pallas kernels: 129 us -> 127 us  [body(): pl.pallas_call(kernel, name='convolve', out_shape=pltpu.VMEM((2, 128, 16,...]
    unnamed x0 -> x1, local copies, waits for them, and re-layouts: none -> 1.32 us
where the time goes in v2:
time: 128 us
  Pallas kernels  127 us (99%)
  local copies, waits for them, and re-layouts  1.32 us (1%)
    pallas_call x1, Pallas kernels, body(): pl.pallas_call(kernel, name='convolve', out_shape=pltpu.VMEM((2, 128, 16,...  127 us

profile of v2, /device:TPU:1, one launch (start us, length us, event | category | flops | bytes accessed | tf_op | source)
XLA Modules:
  0.0 128.1 jit_solution(7309397050759994868)
XLA Ops:
  0.0 126.8 %convolve.1 = f32[2,128,16,128]{3,2,1,0:T(8,128)S(1)} custom-call(f32[2,128,16,128]{3,2,1,0:T(8,128)} %bitcast.11, bf16[2,256,256]{2,1,0:T(8,128)(2,1)} %constant.14.clone.high_far, bf16[2,256,256]{2,1,0:T(8,128)(2,1)} %constant.15.clone.low_far, f32[3,2,128,128]{3,2,1,0:T(8,128)} %constant.16.clone.lanes_far, f32[3,2,128,128]{3,2,1,0:T(8,128)} %constant.17.clone.place_far, ...), custom_call_target="tpu_custom_call" | custom-call | tf_op jit(solution)/shard_map/convolve/pallas_call | solution.py:461
  126.8 1.3 %copy.12 = f32[2,262144]{1,0:T(2,128)} copy(f32[2,262144]{1,0:T(2,128)S(1)} %bitcast.10) | data formatting | bytes 4194304

commit v3 on v2

--- a/solution.py
+++ b/solution.py
@@ -290,9 +290,10 @@
         return pl.ds(first_row, 128, stride=8)
 
     def expand(j, carry):
-        i, h = lax.div(j, 2), lax.rem(j, 2)
-
-        @pl.when(j < 2)
+        i = jnp.where(j < 4, lax.rem(j, 2), 2)
+        h = jnp.where(j < 4, lax.div(j, 2), j - 4)
+
+        @pl.when((j < 4) & (i == 0))
         def _():
             arrived(kept.at[h], h)
 
@@ -314,7 +315,7 @@
                 re, im = times(parts(mixed, w), by)
                 sent_rows[i, h, every(c), :] = re
                 sent_rows[i, h, every(4 + c), :] = im
-        exchange(lambda q: sent.at[i, h, q], lambda p: field.at[i, h, p], 2 + j)
+        exchange(lambda q: sent.at[i, h, q], lambda p: field.at[i, h, p], 2 + 2 * i + h)
         return carry
 
     lax.fori_loop(0, 6, expand, 0)
@@ -394,7 +395,16 @@
                     re, im = parts(mixed, w)
                     back_rows[i, h, every(s), :] = re
                     back_rows[i, h, every(4 + s), :] = im
-            exchange(lambda q: back.at[i, h, q], lambda p: home.at[i, h, p], 8 + 2 * i + h)
+
+            def give(k, within):
+                exchange(
+                    lambda q: back.at[k, h, q], lambda p: home.at[k, h, p], 8 + 2 * k + h
+                )
+                return within
+
+            first_one = jnp.where(h == 0, i, 0)
+            past_last = jnp.where(h == 0, i + 1, jnp.where(i == 2, 3, 0))
+            lax.fori_loop(first_one, past_last, give, 0)
             return inside
 
         lax.fori_loop(0, 2, part, 0)
@@ -403,8 +413,8 @@
     lax.fori_loop(0, 3, middle, 0)
 
     def gather(j, carry):
-        i, h = lax.div(j, 2), lax.rem(j, 2)
-        arrived(home.at[i, h], 8 + j)
+        i, h = lax.rem(j, 3), lax.div(j, 3)
+        arrived(home.at[i, h], 8 + 2 * i + h)
         by_low = start[i, 0], start[i, 1]
         by_high = start[i, 2], start[i, 3]
         for g in range(2):

time: 128 us -> 127 us (level)
  no operation moved by 1% of the time
where the time goes in v3:
time: 127 us
  Pallas kernels  126 us (99%)
  local copies, waits for them, and re-layouts  1.32 us (1%)
    pallas_call x1, Pallas kernels, body(): pl.pallas_call(kernel, name='convolve', out_shape=pltpu.VMEM((2, 128, 16,...  126 us

profile of v3, /device:TPU:1, one launch (start us, length us, event | category | flops | bytes accessed | tf_op | source)
XLA Modules:
  0.0 126.9 jit_solution(12095558381012146955)
XLA Ops:
  0.0 125.6 %convolve.1 = f32[2,128,16,128]{3,2,1,0:T(8,128)S(1)} custom-call(f32[2,128,16,128]{3,2,1,0:T(8,128)} %bitcast.11, bf16[2,256,256]{2,1,0:T(8,128)(2,1)} %constant.14.clone.high_far, bf16[2,256,256]{2,1,0:T(8,128)(2,1)} %constant.15.clone.low_far, f32[3,2,128,128]{3,2,1,0:T(8,128)} %constant.16.clone.lanes_far, f32[3,2,128,128]{3,2,1,0:T(8,128)} %constant.17.clone.place_far, ...), custom_call_target="tpu_custom_call" | custom-call | tf_op jit(solution)/shard_map/convolve/pallas_call | solution.py:471
  125.6 1.3 %copy.12 = f32[2,262144]{1,0:T(2,128)} copy(f32[2,262144]{1,0:T(2,128)S(1)} %bitcast.10) | data formatting | bytes 4194304

commit v4 on v3

--- a/solution.py
+++ b/solution.py
@@ -24,6 +24,21 @@
 
 
 FAR = far_to_near()
+
+
+def paired_steps():
+    order = []
+    for k in range(1, DEVICES):
+        t = (STEP * k) % 128
+        step = (t // 32, t // 16 % 2, t // 4 % 4, t % 4)
+        other = (-step[0] % 4, step[1], -step[2] % 4, -step[3] % 4)
+        for one in (step, other):
+            if one not in order:
+                order.append(one)
+    return order
+
+
+MIX = paired_steps()
 
 MESH = pl.DeviceIdType.MESH
 F32 = jnp.float32
@@ -216,6 +231,10 @@
         for dx, dc, dz, dy in FAR:
             act(to_x[dx] + to_core[dc], to_z[dz] + to_y[dy])
 
+    def by_mix(act):
+        for dx, dc, dz, dy in MIX:
+            act(to_x[dx] + to_core[dc], to_z[dz] + to_y[dy])
+
     barrier = pltpu.get_barrier_semaphore()
 
     def greet(to_row, to_col):
@@ -225,7 +244,7 @@
     loads[0].wait()
     pl.semaphore_wait(barrier, DEVICES - 1)
 
-    def exchange(src_of, dst_of, phase, order=each_peer):
+    def exchange(src_of, dst_of, phase, order=by_mix):
         mine = dst_of(me)
 
         def one(to_row, to_col):

time: 127 us -> 127 us (level)
  no operation moved by 1% of the time
where the time goes in v4:
time: 127 us
  Pallas kernels  125 us (98%)
  local copies, waits for them, and re-layouts  1.32 us (1%)
    pallas_call x1, Pallas kernels, body(): pl.pallas_call(kernel, name='convolve', out_shape=pltpu.VMEM((2, 128, 16,...  125 us

profile of v4, /device:TPU:1, one launch (start us, length us, event | category | flops | bytes accessed | tf_op | source)
XLA Modules:
  0.0 126.7 jit_solution(15686071181154504112)
XLA Ops:
  0.0 125.3 %convolve.1 = f32[2,128,16,128]{3,2,1,0:T(8,128)S(1)} custom-call(f32[2,128,16,128]{3,2,1,0:T(8,128)} %bitcast.11, bf16[2,256,256]{2,1,0:T(8,128)(2,1)} %constant.14.clone.high_far, bf16[2,256,256]{2,1,0:T(8,128)(2,1)} %constant.15.clone.low_far, f32[3,2,128,128]{3,2,1,0:T(8,128)} %constant.16.clone.lanes_far, f32[3,2,128,128]{3,2,1,0:T(8,128)} %constant.17.clone.place_far, ...), custom_call_target="tpu_custom_call" | custom-call | tf_op jit(solution)/shard_map/convolve/pallas_call | solution.py:490
  125.3 1.3 %copy.12 = f32[2,262144]{1,0:T(2,128)} copy(f32[2,262144]{1,0:T(2,128)S(1)} %bitcast.10) | data formatting | bytes 4194304

commit v5 on v3

--- a/solution.py
+++ b/solution.py
@@ -441,12 +441,16 @@
                     for r in range(2):
                         final_rows[h, every(1024 * f + 2 * c + r), :] = total[h, c, f, r]
             some = pl.ds(pl.multiple_of(8 * h, 8), 8)
-            exchange(
-                lambda q: final.at[h, pl.ds(2 * q, 2)],
-                lambda p: out.at[:, p, some],
-                14 + h,
-                far_first,
-            )
+            def give(order):
+                exchange(
+                    lambda q: final.at[h, pl.ds(2 * q, 2)],
+                    lambda p: out.at[:, p, some],
+                    14 + h,
+                    order,
+                )
+
+            pl.when(h == 0)(functools.partial(give, each_peer))
+            pl.when(h == 1)(functools.partial(give, far_first))
 
         return carry
 

time: 127 us -> 127 us (level)
  no operation moved by 1% of the time
where the time goes in v5:
time: 127 us
  Pallas kernels  126 us (99%)
  local copies, waits for them, and re-layouts  1.32 us (1%)
    pallas_call x1, Pallas kernels, body(): pl.pallas_call(kernel, name='convolve', out_shape=pltpu.VMEM((2, 128, 16,...  126 us

profile of v5, /device:TPU:1, one launch (start us, length us, event | category | flops | bytes accessed | tf_op | source)
XLA Modules:
  0.0 127.0 jit_solution(3184880562068620222)
XLA Ops:
  0.0 125.7 %convolve.1 = f32[2,128,16,128]{3,2,1,0:T(8,128)S(1)} custom-call(f32[2,128,16,128]{3,2,1,0:T(8,128)} %bitcast.11, bf16[2,256,256]{2,1,0:T(8,128)(2,1)} %constant.14.clone.high_far, bf16[2,256,256]{2,1,0:T(8,128)(2,1)} %constant.15.clone.low_far, f32[3,2,128,128]{3,2,1,0:T(8,128)} %constant.16.clone.lanes_far, f32[3,2,128,128]{3,2,1,0:T(8,128)} %constant.17.clone.place_far, ...), custom_call_target="tpu_custom_call" | custom-call | tf_op jit(solution)/shard_map/convolve/pallas_call | solution.py:475
  125.7 1.3 %copy.12 = f32[2,262144]{1,0:T(2,128)} copy(f32[2,262144]{1,0:T(2,128)S(1)} %bitcast.10) | data formatting | bytes 4194304
